TPU v7x, 32 devices: a whole 2x2x4 slice. The times are simulated.
32 devices in a mesh: fsdp: 8 (over z, y), tensor: 4 (over x, core).
Axes of the slice: x: 2, y: 2, z: 4, core: 2. Of those that a mesh axis runs over, the one named last changes fastest.
Arguments:
- tokens: bfloat16 [12288, 768], P(('fsdp', 'tensor')), may hold values from -6 to 6
- attn_weight: bfloat16 [3, 768, 768], P(None, 'fsdp', 'tensor'), may hold values from -0.21875 to 0.21875
- query_value_bias: bfloat16 [2, 12, 64], P(None, 'tensor', 'fsdp'), may hold values from -3 to 3
- out_weight: bfloat16 [768, 768], P('tensor', 'fsdp'), may hold values from -1.25 to 1.25
- hidden_weight: bfloat16 [768, 3072], P('fsdp', 'tensor'), may hold values from -0.21875 to 0.21875
- hidden_bias: bfloat16 [48, 64], P('tensor', 'fsdp'), may hold values from -3 to 3
- down_weight: bfloat16 [3072, 768], P('tensor', 'fsdp'), may hold values from -0.109375 to 0.109375
- norm_gains: bfloat16 [2, 768], P(None, 'fsdp'), may hold values from 0.5 to 1.5
- norm_biases: bfloat16 [2, 768], P(None, 'fsdp'), may hold values from -2 to 2
- output_biases: bfloat16 [2, 768], P(None, 'fsdp'), may hold values from -2 to 2
- segment_ids: int32 [12288], P('fsdp'), may hold values from 0 to 15, as said below
- padding: int32 [12288], P('fsdp'), may hold values from 0 to 1, as said below
- cotangent: bfloat16 [12288, 768], P(('fsdp', 'tensor')), may hold values from -6 to 6
Outputs:
- layer_out: bfloat16 [12288, 768], P(('fsdp', 'tensor'))
- tokens_grad: float32 [12288, 768], P(('fsdp', 'tensor'))
- attn_weight_grad: float32 [3, 768, 768], P(None, 'fsdp', 'tensor')
- query_value_bias_grad: float32 [2, 12, 64], P(None, 'tensor', 'fsdp')
- out_weight_grad: float32 [768, 768], P('tensor', 'fsdp')
- hidden_weight_grad: float32 [768, 3072], P('fsdp', 'tensor')
- hidden_bias_grad: float32 [48, 64], P('tensor', 'fsdp')
- down_weight_grad: float32 [3072, 768], P('tensor', 'fsdp')
- norm_gains_grad: float32 [2, 768], P(None, 'fsdp')
- norm_biases_grad: float32 [2, 768], P(None, 'fsdp')
- output_biases_grad: float32 [2, 768], P(None, 'fsdp')
- root_squares: float32 [3], replicated
Inputs may be any that keep to these rules, and one draw needn't show every extreme that they name: `segment_ids`: within each sequence of 1536 positions, segment ids start at 0 and rise by one at each new document; every document has 96 to 768 tokens except the last of a sequence, which its end may cut; some document has exactly 768 tokens. Within each sequence, the padding positions (value 0) form a tail of at most 192 positions.
All inputs are finite; a program needn't handle non-finite values.
Results may differ from a plain program's by a relative error of at most 0.013.
The roundings to bfloat16 on the way count: a program that leaves them out, or rounds other values in their place, can miss the bound.
Values may be sent and summed in bfloat16 or wider, within the bound.
A program may use at most 192 MiB of HBM per device.

v0:
```python
import jax
import jax.numpy as jnp
from jax import lax
from jax.sharding import PartitionSpec as P

D = 768
DH = 64


EPSILON = 1e-12


def split_up(value, dim, devices):
    before, after = (value.shape[:dim], value.shape[dim + 1 :])
    return jnp.moveaxis(value.reshape(*before, devices, -1, *after), dim, 0)


def summed_on_arrival(value, axis, dim):
    blocks = split_up(value, dim, lax.axis_size(axis))
    arrived = lax.all_to_all(blocks, axis, split_axis=0, concat_axis=0, tiled=True)
    return arrived.astype(jnp.float32).sum(axis=0)


def sent_together(arrays, axis, dim, along):
    ends, at = ([], 0)
    for a in arrays[:-1]:
        at += a.shape[along]
        ends.append(at)
    both = jnp.concatenate(arrays, axis=along)
    return tuple(jnp.split(summed_on_arrival(both, axis, dim), ends, axis=along))


def layer_norm(hidden, gain_row, shift_row):
    row_mean = jnp.mean(hidden, axis=-1, keepdims=True)
    centered = hidden - row_mean
    variance = jnp.mean(centered * centered, axis=-1, keepdims=True)
    return centered * lax.rsqrt(variance + EPSILON) * gain_row + shift_row


def gelu_exact(value):
    return jax.nn.gelu(value, approximate=False)


def shards(
    tokens,
    attn_weight,
    query_value_bias,
    out_weight,
    hidden_weight,
    hidden_bias,
    down_weight,
    norm_gains,
    norm_biases,
    output_biases,
    segment_ids,
    padding,
    cotangent,
):
    wide = jnp.float32
    narrow = jnp.bfloat16
    gathered = (
        lax.all_gather(attn_weight, "fsdp", axis=1, tiled=True),
        lax.all_gather(query_value_bias, "fsdp", axis=2, tiled=True),
        lax.all_gather(out_weight, "fsdp", axis=1, tiled=True),
        lax.all_gather(hidden_weight, "fsdp", axis=0, tiled=True),
        lax.all_gather(hidden_bias, "fsdp", axis=1, tiled=True),
        lax.all_gather(down_weight, "fsdp", axis=1, tiled=True),
        lax.all_gather(norm_gains, "fsdp", axis=1, tiled=True),
        lax.all_gather(norm_biases, "fsdp", axis=1, tiled=True),
        lax.all_gather(output_biases, "fsdp", axis=1, tiled=True),
    )
    w_qkv, qv_full, w_proj, w_up, up_bias, w_down, gain_rows, shift_rows, bias_rows = gathered
    row_count = tokens.shape[0]
    seq_len = segment_ids.shape[0]
    tensor_place = lax.axis_index("tensor")
    local_pad = lax.dynamic_slice_in_dim(padding, tensor_place * row_count, row_count, 0).astype(
        wide
    )
    whole_rows = lax.all_gather(tokens, "tensor", axis=0, tiled=True)
    width = w_qkv.shape[2]
    heads = width // DH
    projected = jnp.einsum("sd,jde->jse", whole_rows, w_qkv, preferred_element_type=wide)
    qv_flat = qv_full.astype(wide).reshape(2, width)
    queries = (projected[0] + qv_flat[0]).astype(narrow).reshape(seq_len, heads, DH)
    all_keys = projected[1].astype(narrow).reshape(seq_len, heads, DH)
    all_values = (projected[2] + qv_flat[1]).astype(narrow).reshape(seq_len, heads, DH)
    block_rows = min(512, seq_len)
    block_count = seq_len // block_rows
    positions = jnp.arange(seq_len, dtype=jnp.int32)
    key_live = padding == 1

    def scores_of(row_start):
        q_rows = lax.dynamic_slice_in_dim(queries, row_start, block_rows, 0)
        seg_rows = lax.dynamic_slice_in_dim(segment_ids, row_start, block_rows, 0)
        pos_rows = row_start + jnp.arange(block_rows, dtype=jnp.int32)
        allowed = (seg_rows[:, None] == segment_ids[None, :]) & key_live[None, :] | (
            pos_rows[:, None] == positions[None, :]
        )
        raw_scores = (
            jnp.einsum("qhd,khd->hqk", q_rows, all_keys, preferred_element_type=wide) * 0.125
        )
        return (q_rows, jnp.where(allowed[None], raw_scores, -1e30))

    def forward_block(block_index):
        row_start = block_index * block_rows
        q_rows, masked = scores_of(row_start)
        row_top = jnp.max(masked, axis=-1, keepdims=True)
        exp_terms = jnp.exp(masked - row_top)
        row_total = jnp.sum(exp_terms, axis=-1, keepdims=True)
        attn_probs = exp_terms / row_total
        pad_rows = lax.dynamic_slice_in_dim(padding, row_start, block_rows, 0).astype(wide)
        context = jnp.einsum(
            "hqk,khd->qhd", attn_probs.astype(narrow), all_values, preferred_element_type=wide
        )
        return (context * pad_rows[:, None, None], row_top[..., 0] + jnp.log(row_total[..., 0]))

    block_ids = jnp.arange(block_count, dtype=jnp.int32)
    contexts, log_totals = lax.map(forward_block, block_ids)
    context_low = contexts.reshape(seq_len, width).astype(narrow)
    attn_part = jnp.dot(context_low, w_proj, preferred_element_type=wide)
    attn_branch = lax.psum_scatter(
        attn_part, "tensor", scatter_dimension=0, tiled=True
    ) + bias_rows[0].astype(wide)
    input_rows = tokens.astype(wide)
    first_norm, first_pull = jax.vjp(
        layer_norm, input_rows + attn_branch, gain_rows[0].astype(wide), shift_rows[0].astype(wide)
    )
    up_use, down_use, up_bias_use = (w_up, w_down, up_bias)
    normed_all = lax.all_gather(first_norm.astype(narrow), "tensor", axis=0, tiled=True)
    pre_act = jnp.dot(normed_all, up_use, preferred_element_type=wide) + up_bias_use.astype(
        wide
    ).reshape(-1)
    acted, gelu_pull = jax.vjp(gelu_exact, pre_act)
    acted_low = acted.astype(narrow)
    ff_part = jnp.dot(acted_low, down_use, preferred_element_type=wide)
    ff_sum = lax.psum_scatter(
        ff_part.astype(jnp.bfloat16), "tensor", scatter_dimension=0, tiled=True
    ).astype(jnp.float32)
    ff_branch = ff_sum + bias_rows[1].astype(wide)
    layer_value, second_pull = jax.vjp(
        layer_norm, first_norm + ff_branch, gain_rows[1].astype(wide), shift_rows[1].astype(wide)
    )
    layer_out = layer_value.astype(narrow)
    live_col = local_pad[:, None]
    squares = jnp.stack(
        [
            jnp.sum(live_col * input_rows * input_rows),
            jnp.sum(live_col * attn_branch * attn_branch),
            jnp.sum(live_col * ff_branch * ff_branch),
        ]
    )
    square_sums, live_count = lax.psum((squares, jnp.sum(local_pad)), ("fsdp", "tensor"))
    root_values = jnp.sqrt(square_sums / (live_count * D))
    d_second, d_gain_two, d_shift_two = second_pull(cotangent.astype(wide))
    d_ff_low = d_second.astype(narrow)
    d_ff_bias = jnp.sum(d_ff_low.astype(wide), axis=0)
    d_ff_all = lax.all_gather(d_ff_low, "tensor", axis=0, tiled=True)
    d_down = jnp.einsum("sf,sd->fd", acted_low, d_ff_all, preferred_element_type=wide)
    d_acted = jnp.einsum("sd,fd->sf", d_ff_all, down_use, preferred_element_type=wide)
    d_pre_low = gelu_pull(d_acted)[0].astype(narrow)
    d_up_bias = jnp.sum(d_pre_low.astype(wide), axis=0).reshape(up_bias_use.shape)
    d_up = jnp.einsum("sd,sf->df", normed_all, d_pre_low, preferred_element_type=wide)
    d_norm_part = jnp.einsum("sf,df->sd", d_pre_low, up_use, preferred_element_type=wide)
    d_first_in = d_second + lax.psum_scatter(d_norm_part, "tensor", scatter_dimension=0, tiled=True)
    d_first, d_gain_one, d_shift_one = first_pull(d_first_in)
    d_attn_low = d_first.astype(narrow)
    d_attn_bias = jnp.sum(d_attn_low.astype(wide), axis=0)
    d_attn_all = lax.all_gather(d_attn_low, "tensor", axis=0, tiled=True)
    d_proj = jnp.einsum("se,sd->ed", context_low, d_attn_all, preferred_element_type=wide)
    d_context = jnp.einsum("sd,ed->se", d_attn_all, w_proj, preferred_element_type=wide).astype(
        narrow
    )
    d_context = d_context.reshape(seq_len, heads, DH)

    def backward_block(carried, block_index):
        d_keys_sum, d_values_sum = carried
        row_start = block_index * block_rows
        q_rows, masked = scores_of(row_start)
        attn_probs = jnp.exp(masked - log_totals[block_index][..., None])
        pad_rows = lax.dynamic_slice_in_dim(padding, row_start, block_rows, 0).astype(narrow)
        d_ctx_rows = (
            lax.dynamic_slice_in_dim(d_context, row_start, block_rows, 0) * pad_rows[:, None, None]
        )
        d_probs = jnp.einsum("qhd,khd->hqk", d_ctx_rows, all_values, preferred_element_type=wide)
        d_values_sum = d_values_sum + jnp.einsum(
            "hqk,qhd->khd", attn_probs.astype(narrow), d_ctx_rows, preferred_element_type=wide
        )
        inner_sum = jnp.sum(attn_probs * d_probs, axis=-1, keepdims=True)
        d_scores = (attn_probs * (d_probs - inner_sum)).astype(narrow)
        d_query_rows = (
            jnp.einsum("hqk,khd->qhd", d_scores, all_keys, preferred_element_type=wide) * 0.125
        )
        d_keys_sum = (
            d_keys_sum
            + jnp.einsum("hqk,qhd->khd", d_scores, q_rows, preferred_element_type=wide) * 0.125
        )
        return ((d_keys_sum, d_values_sum), d_query_rows)

    zero_heads = jnp.zeros((seq_len, heads, DH), wide)
    (d_keys_all, d_values_all), d_query_blocks = lax.scan(
        backward_block, (zero_heads, zero_heads), block_ids
    )
    d_qkv = jnp.stack(
        [
            d_query_blocks.reshape(seq_len, width),
            d_keys_all.reshape(seq_len, width),
            d_values_all.reshape(seq_len, width),
        ]
    ).astype(narrow)
    d_qkv_wide = d_qkv.astype(wide)
    d_qv_bias = jnp.stack([jnp.sum(d_qkv_wide[0], axis=0), jnp.sum(d_qkv_wide[2], axis=0)]).reshape(
        2, heads, DH
    )
    d_attn_weight = jnp.einsum("sd,jse->jde", whole_rows, d_qkv, preferred_element_type=wide)
    d_tokens_part = jnp.einsum("jse,jde->sd", d_qkv, w_qkv, preferred_element_type=wide)
    d_tokens = d_first + lax.psum_scatter(
        d_tokens_part.astype(jnp.bfloat16), "tensor", scatter_dimension=0, tiled=True
    ).astype(jnp.float32)
    gain_terms, shift_terms, bias_terms = lax.psum(
        (
            jnp.stack([d_gain_one, d_gain_two]),
            jnp.stack([d_shift_one, d_shift_two]),
            jnp.stack([d_attn_bias, d_ff_bias]),
        ),
        "tensor",
    )
    grads = (
        summed_on_arrival(d_attn_weight.astype(jnp.bfloat16), "fsdp", 1),
        summed_on_arrival(d_qv_bias.astype(jnp.bfloat16), "fsdp", 2),
        summed_on_arrival(d_proj.astype(jnp.bfloat16), "fsdp", 1),
        summed_on_arrival(d_up.astype(jnp.bfloat16), "fsdp", 0),
        summed_on_arrival(d_up_bias.astype(jnp.bfloat16), "fsdp", 1),
        *sent_together(
            (
                d_down.astype(jnp.bfloat16),
                gain_terms.astype(jnp.bfloat16),
                shift_terms.astype(jnp.bfloat16),
                bias_terms.astype(jnp.bfloat16),
            ),
            "fsdp",
            1,
            0,
        ),
    )
    return (
        layer_out,
        d_tokens,
        grads[0],
        grads[1],
        grads[2],
        grads[3],
        grads[4],
        grads[5],
        grads[6],
        grads[7],
        grads[8],
        root_values,
    )


def solution(mesh):
    placed = (
        P(("fsdp", "tensor"), None),
        P(None, "fsdp", "tensor"),
        P(None, "tensor", "fsdp"),
        P("tensor", "fsdp"),
        P("fsdp", "tensor"),
        P("tensor", "fsdp"),
        P("tensor", "fsdp"),
        P(None, "fsdp"),
        P(None, "fsdp"),
        P(None, "fsdp"),
        P("fsdp"),
        P("fsdp"),
        P(("fsdp", "tensor"), None),
    )
    return jax.shard_map(
        shards,
        mesh=mesh,
        in_specs=placed,
        out_specs=(
            P(("fsdp", "tensor"), None),
            P(("fsdp", "tensor"), None),
            P(None, "fsdp", "tensor"),
            P(None, "tensor", "fsdp"),
            P("tensor", "fsdp"),
            P("fsdp", "tensor"),
            P("tensor", "fsdp"),
            P("tensor", "fsdp"),
            P(None, "fsdp"),
            P(None, "fsdp"),
            P(None, "fsdp"),
            P(),
        ),
        check_vma=False,
    )
```

profile of v0, /device:TPU:0, one launch (start us, length us, event | category | flops | bytes accessed | tf_op | source)
XLA Modules:
  0.0 711.6 jit_solution(12690553113881603985)
XLA Ops:
  9.6 32.2 %all_gather.41 = bf16[2,3,64]{1,0,2:T(2,128)(2,1)S(1)} all-gather(bf16[2,3,8]{1,0,2:T(2,128)(2,1)S(1)} %copy.145), channel_id=1, replica_groups=mesh['fsdp'=8,'tensor'=4] {'fsdp'}, dimensions={2}, use_global_device_ids=true | all-gather | bytes 864 | tf_op jit(solution)/shard_map/all_gather | solution.py:63
  43.9 31.5 %all_gather.42 = bf16[192,768]{0,1:T(8,128)(2,1)S(1)} all-gather(bf16[192,96]{0,1:T(8,128)(2,1)S(1)} %copy.149), channel_id=1, replica_groups=mesh['fsdp'=8,'tensor'=4] {'fsdp'}, dimensions={1}, use_global_device_ids=true | all-gather | bytes 331776 | tf_op jit(solution)/shard_map/all_gather | solution.py:64
  76.2 37.9 %all_gather.39 = bf16[3,768,192]{2,0,1:T(4,128)(2,1)} all-gather(bf16[3,96,192]{2,0,1:T(4,128)(2,1)S(1)} %copy.143), channel_id=1, replica_groups=mesh['fsdp'=8,'tensor'=4] {'fsdp'}, dimensions={1}, use_global_device_ids=true | all-gather | bytes 995328 | tf_op jit(solution)/shard_map/all_gather | solution.py:62
  119.3 34.3 %while.28 = (s32[]{:T(128)}, bf16[3,512,3,64]{1,3,2,0:T(8,128)(2,1)S(1)}, f32[3,3,512]{2,1,0:T(4,128)}, s32[3]{0:T(128)S(1)}, s32[1536]{0:T(1024)S(1)}, /*index=...) while((s32[]{:T(128)}, ...), condition=%wide.region_3.4_spmd.clone, body=%wide.region_0.3_spmd.clone.sunk | while | flops 635534848 | bytes 33306336 | solution.py:118
  158.8 17.7 %all-gather.1 = bf16[8,96,2]{1,2,0:T(2,128)(2,1)S(1)} all-gather(bf16[1,96,2]{1,2,0:T(2,128)(2,1)S(1)} %bitcast.168), channel_id=1, replica_groups=mesh['fsdp'=8,'tensor'=4] {'fsdp'}, dimensions={0}, use_global_device_ids=true | all-gather | bytes 3456 | tf_op jit(solution)/shard_map/all_gather | solution.py:68
  176.6 16.6 %all-gather.2 = bf16[8,96,2]{1,2,0:T(2,128)(2,1)S(1)} all-gather(bf16[1,96,2]{1,2,0:T(2,128)(2,1)S(1)} %bitcast.169), channel_id=1, replica_groups=mesh['fsdp'=8,'tensor'=4] {'fsdp'}, dimensions={0}, use_global_device_ids=true | all-gather | bytes 3456 | tf_op jit(solution)/shard_map/all_gather | solution.py:69
  193.3 17.7 %all-gather = bf16[8,96,2]{1,2,0:T(2,128)(2,1)S(1)} all-gather(bf16[1,96,2]{1,2,0:T(2,128)(2,1)S(1)} %bitcast.170), channel_id=1, replica_groups=mesh['fsdp'=8,'tensor'=4] {'fsdp'}, dimensions={0}, use_global_device_ids=true | all-gather | bytes 3456 | tf_op jit(solution)/shard_map/all_gather | solution.py:70
  215.4 26.5 %all_gather.48 = bf16[12,64]{0,1:T(8,128)(2,1)S(1)} all-gather(bf16[12,8]{0,1:T(8,128)(2,1)S(1)} %copy-done.37), channel_id=1, replica_groups=mesh['fsdp'=8,'tensor'=4] {'fsdp'}, dimensions={1}, use_global_device_ids=true | all-gather | bytes 1728 | tf_op jit(solution)/shard_map/all_gather | solution.py:66
  242.1 15.1 %multiply_convert_fusion.1 = (bf16[1536,768]{1,0:T(8,128)(2,1)}, f32[1536,768]{1,0:T(8,128)}, f32[1536,768]{1,0:T(8,128)}) fusion(f32[768]{0:T(1024)S(1)} %reshape.337, bf16[1536,768]{1,0:T(8,128)(2,1)} %all-gather.12.cloned.1.call-done, bf16[768,768]{1,0:T(8,128)(2,1)} %all-gather.14.cloned.1.call-done), kind=kOutput, calls=%fused_computation.53 | convolution fusion | flops 1889796096 | bytes 15338496 | tf_op jit(solution)/shard_map/dot_general | solution.py:130
  257.1 22.6 %all-gather.16.cloned.1.call-done = bf16[768,768]{0,1:T(8,128)(2,1)} async-done(((bf16[768,96]{0,1:T(8,128)(2,1)}), bf16[768,768]{0,1:T(8,128)(2,1)}) %all-gather.16.cloned.1.call-update) | async-done | bytes 1179664 | tf_op jit(solution)/shard_map/all_gather | solution.py:67
  285.9 30.8 %reduce-scatter.7.cloned.1.call-done = bf16[384,768]{1,0:T(8,128)(2,1)} async-done(((bf16[1536,768]{1,0:T(8,128)(2,1)}), bf16[384,768]{1,0:T(8,128)(2,1)}) %reduce-scatter.7.cloned.1.call-update) | async-done | bytes 589840 | tf_op jit(solution)/shard_map/reduce_scatter | solution.py:136
  325.8 23.8 %all-gather.18.cloned.1.call-done = bf16[1536,768]{1,0:T(8,128)(2,1)} async-done(((bf16[384,768]{1,0:T(8,128)(2,1)}), bf16[1536,768]{1,0:T(8,128)(2,1)}) %all-gather.18.cloned.1.call-update) | async-done | bytes 2359312 | tf_op jit(solution)/shard_map/all_gather | solution.py:157
  349.6 8.7 %fusion.74 = (bf16[768]{0:T(1024)(128)(2,1)}, bf16[1536,768]{1,0:T(8,128)(2,1)S(1)}) fusion(f32[1536,768]{1,0:T(8,128)} %get-tuple-element.383, f32[1536,768]{1,0:T(8,128)} %get-tuple-element.400, f32[768]{0:T(1024)} %copy-done.35, bf16[1536,768]{1,0:T(8,128)(2,1)} %all-gather.18.cloned.1.call-done, bf16[768,768]{0,1:T(8,128)(2,1)} %all-gather.16.cloned.1.call-done), kind=kOutput, calls=%fused_computation.158 | convolution fusion | flops 1830812928 | bytes 15340032 | tf_op jit(solution)/shard_map/sd,fd->sf/dot_general | solution.py:159
  364.1 48.0 %reduce-scatter.9.cloned.1.call-done = f32[384,768]{1,0:T(8,128)} async-done(((f32[1536,768]{1,0:T(8,128)}), f32[384,768]{1,0:T(8,128)}) %reduce-scatter.9.cloned.1.call-update) | async-done | bytes 1179664 | tf_op jit(solution)/shard_map/reduce_scatter | solution.py:164
  440.6 11.6 %all-reduce.1 = (bf16[2,768]{1,0:T(2,128)(2,1)}, bf16[2,768]{1,0:T(2,128)(2,1)}, bf16[2,768]{1,0:T(2,128)(2,1)}) all-reduce(f32[2,768]{1,0:T(2,128)} %pad_maximum_fusion.4, f32[2,768]{1,0:T(2,128)} %pad_maximum_fusion.3, f32[2,768]{1,0:T(2,128)} %pad_maximum_fusion.2), channel_id=1, replica_groups=mesh['fsdp'=8,'tensor'=4] {'tensor'}, use_global_device_ids=true, to_apply=%region_35.36 | all-reduce | flops 4608 | bytes 27648 | tf_op jit(solution)/shard_map/psum | solution.py:219
  462.8 101.5 %while.29 = (s32[]{:T(128)}, f32[1536,3,64]{0,2,1:T(8,128)S(1)}, f32[1536,3,64]{0,2,1:T(8,128)S(1)}, bf16[3,512,3,64]{1,3,2,0:T(8,128)(2,1)}, s32[3]{0:T(128)S(1...) while((s32[]{:T(128)}, f32[1536,3,64]{0,2,1:T(8,128)S(1)}, ...), condition=%wide.region_17.18_spmd.clone, body=%wide.region_15.17_spmd.clone.sunk | while | flops 1536687616 | bytes 141431936 | solution.py:200
  470.9 7.2 %multiply_reduce_fusion.6 = (f32[3,512]{1,0:T(4,128)S(1)}, f32[3,512,1536]{2,1,0:T(8,128)}) fusion(f32[3,512,1536]{2,1,0:T(8,128)S(1)} %fusion.142, f32[3,512]{1,0:T(4,128)S(1)} %dynamic-slice_bitcast_fusion.2, bf16[1536,3,64]{0,2,1:T(8,128)(2,1)S(1)} %get-tuple-element.637, bf16[1536,3,64]{0,2,1:T(8,128)(2,1)} %get-tuple-element.634, ...), kind=kOutput, calls=%fused_computation.22.clone.1 | convolution fusion | flops 313784832 | bytes 20459524 | tf_op jit(solution)/shard_map/while/body/eval_jaxpr/qhd,khd->hqk/dot_general | solution.py:100
  478.2 9.4 %multiply_convert_fusion.3 = bf16[3,512,1536]{2,1,0:T(8,128)(2,1)} fusion(f32[3,512,1536]{2,1,0:T(8,128)} %get-tuple-element.549, f32[3,512,1536]{2,1,0:T(8,128)} %copy-done, f32[3,512]{1,0:T(4,128)S(1)} %get-tuple-element.550), kind=kLoop, calls=%fused_computation.21.clone.1 | loop fusion | flops 7077888 | bytes 23599104 | tf_op jit(solution)/shard_map/while/body/eval_jaxpr/convert_element_type | solution.py:189
  504.8 7.2 %multiply_reduce_fusion.6 = (f32[3,512]{1,0:T(4,128)S(1)}, f32[3,512,1536]{2,1,0:T(8,128)}) fusion(f32[3,512,1536]{2,1,0:T(8,128)S(1)} %fusion.142, f32[3,512]{1,0:T(4,128)S(1)} %dynamic-slice_bitcast_fusion.2, bf16[1536,3,64]{0,2,1:T(8,128)(2,1)S(1)} %get-tuple-element.637, bf16[1536,3,64]{0,2,1:T(8,128)(2,1)} %get-tuple-element.634, ...), kind=kOutput, calls=%fused_computation.22.clone.1 | convolution fusion | flops 313784832 | bytes 20459524 | tf_op jit(solution)/shard_map/while/body/eval_jaxpr/qhd,khd->hqk/dot_general | solution.py:100
  512.0 9.4 %multiply_convert_fusion.3 = bf16[3,512,1536]{2,1,0:T(8,128)(2,1)} fusion(f32[3,512,1536]{2,1,0:T(8,128)} %get-tuple-element.549, f32[3,512,1536]{2,1,0:T(8,128)} %copy-done, f32[3,512]{1,0:T(4,128)S(1)} %get-tuple-element.550), kind=kLoop, calls=%fused_computation.21.clone.1 | loop fusion | flops 7077888 | bytes 23599104 | tf_op jit(solution)/shard_map/while/body/eval_jaxpr/convert_element_type | solution.py:189
  538.6 7.2 %multiply_reduce_fusion.6 = (f32[3,512]{1,0:T(4,128)S(1)}, f32[3,512,1536]{2,1,0:T(8,128)}) fusion(f32[3,512,1536]{2,1,0:T(8,128)S(1)} %fusion.142, f32[3,512]{1,0:T(4,128)S(1)} %dynamic-slice_bitcast_fusion.2, bf16[1536,3,64]{0,2,1:T(8,128)(2,1)S(1)} %get-tuple-element.637, bf16[1536,3,64]{0,2,1:T(8,128)(2,1)} %get-tuple-element.634, ...), kind=kOutput, calls=%fused_computation.22.clone.1 | convolution fusion | flops 313784832 | bytes 20459524 | tf_op jit(solution)/shard_map/while/body/eval_jaxpr/qhd,khd->hqk/dot_general | solution.py:100
  545.8 9.4 %multiply_convert_fusion.3 = bf16[3,512,1536]{2,1,0:T(8,128)(2,1)} fusion(f32[3,512,1536]{2,1,0:T(8,128)} %get-tuple-element.549, f32[3,512,1536]{2,1,0:T(8,128)} %copy-done, f32[3,512]{1,0:T(4,128)S(1)} %get-tuple-element.550), kind=kLoop, calls=%fused_computation.21.clone.1 | loop fusion | flops 7077888 | bytes 23599104 | tf_op jit(solution)/shard_map/while/body/eval_jaxpr/convert_element_type | solution.py:189
  583.4 30.8 %all-to-all-done.5 = bf16[8,774,96]{1,2,0:T(8,128)(2,1)S(1)} async-done(((bf16[8,774,96]{1,2,0:T(8,128)(2,1)}), bf16[8,774,96]{1,2,0:T(8,128)(2,1)S(1)}, u32[]{:S(2)}, u32[]{:S(2)}) %all-to-all-start.5) | async-done | bytes 1188896 | tf_op jit(solution)/shard_map/all_to_all | solution.py:20
  645.0 45.4 %all-reduce = (f32[3]{0:T(128)S(1)}, f32[]{:T(128)}) all-reduce(f32[3]{0:T(128)S(1)} %pad_maximum_fusion.5, f32[]{:T(128)} %get-tuple-element.367), channel_id=1, replica_groups=mesh['fsdp'=8,'tensor'=4] {'fsdp','tensor'}, use_global_device_ids=true, to_apply=%region_40.41 | all-reduce | flops 4 | bytes 32 | tf_op jit(solution)/shard_map/psum | solution.py:152
  (327 shorter events, 217.4 us)
Async XLA Ops:
  8.0 106.1 %all-gather.10.cloned.1.call-start = ((), (), s32[]{:S(2)}) async-start(), calls=%async_computation.10 | async-start | bytes 2949120 | tf_op jit(solution)/shard_map/all_gather | solution.py:79
  8.7 203.1 %reduce-scatter.5.cloned.1.call-start = ((), (), s32[]{:S(2)}) async-start(), calls=%async_computation.11 | async-start | bytes 5898240 | tf_op jit(solution)/shard_map/reduce_scatter | solution.py:121
  75.5 78.8 %copy-start.6 = (bf16[192,768]{0,1:T(8,128)(2,1)}, bf16[192,768]{0,1:T(8,128)(2,1)S(1)}, u32[]{:S(2)}) copy-start(bf16[192,768]{0,1:T(8,128)(2,1)S(1)} %all_gather.42) | copy-start | bytes 884740
  158.1 18.5 %copy-start.39 = (bf16[2,96]{1,0:T(2,128)(2,1)S(1)}, bf16[2,96]{1,0:T(2,128)(2,1)}, u32[]{:S(2)}) copy-start(bf16[2,96]{1,0:T(2,128)(2,1)} %param.25) | copy-start | bytes 1156
  158.1 35.2 %copy-start.40 = (bf16[2,96]{1,0:T(2,128)(2,1)S(1)}, bf16[2,96]{1,0:T(2,128)(2,1)}, u32[]{:S(2)}) copy-start(bf16[2,96]{1,0:T(2,128)(2,1)} %param.26) | copy-start | bytes 1156
  158.1 53.7 %copy-start.5 = (bf16[384,768]{1,0:T(8,128)(2,1)S(1)}, bf16[384,768]{1,0:T(8,128)(2,1)}, u32[]{:S(2)}) copy-start(bf16[384,768]{1,0:T(8,128)(2,1)} %param.17) | copy-start | bytes 1769476
  158.1 83.9 %all-gather.14.cloned.1.call-start = ((), (), s32[]{:S(2)}) async-start(), calls=%async_computation.13 | async-start | bytes 1327104 | tf_op jit(solution)/shard_map/all_gather | solution.py:65
  158.7 83.3 %all-gather.12.cloned.1.call-start = ((), (), s32[]{:S(2)}) async-start(), calls=%async_computation.12 | async-start | bytes 2949120 | tf_op jit(solution)/shard_map/all_gather | solution.py:129
  211.8 108.4 %copy-start.23 = (f32[768]{0:T(1024)}, f32[768]{0:T(1024)S(1)}, u32[]{:S(2)}) copy-start(f32[768]{0:T(1024)S(1)} %get-tuple-element.307) | copy-start | bytes 9220
  213.4 103.4 %copy-start.21 = (f32[384]{0:T(512)}, f32[384]{0:T(512)S(1)}, u32[]{:S(2)}) copy-start(f32[384]{0:T(512)S(1)} %broadcast_multiply_fusion.1) | copy-start | bytes 4612
  213.7 103.1 %copy-start.22 = (f32[384]{0:T(512)}, f32[384]{0:T(512)S(1)}, u32[]{:S(2)}) copy-start(f32[384]{0:T(512)S(1)} %fusion.70) | copy-start | bytes 4612
  214.8 64.9 %all-gather.16.cloned.1.call-start = ((), (), s32[]{:S(2)}) async-start(), calls=%async_computation.14 | async-start | bytes 1327104 | tf_op jit(solution)/shard_map/all_gather | solution.py:67
  215.4 101.4 %reduce-scatter.7.cloned.1.call-start = ((), (), s32[]{:S(2)}) async-start(), calls=%async_computation.15 | async-start | bytes 2949120 | tf_op jit(solution)/shard_map/reduce_scatter | solution.py:136
  285.2 64.5 %all-gather.18.cloned.1.call-start = ((), (), s32[]{:S(2)}) async-start(), calls=%async_computation.16 | async-start | bytes 2949120 | tf_op jit(solution)/shard_map/all_gather | solution.py:157
  325.6 86.5 %reduce-scatter.9.cloned.1.call-start = ((), (), s32[]{:S(2)}) async-start(), calls=%async_computation.17 | async-start | bytes 5898240 | tf_op jit(solution)/shard_map/reduce_scatter | solution.py:164
  364.0 88.2 %all-gather.20.cloned.1.call-start = ((), (), s32[]{:S(2)}) async-start(), calls=%async_computation.18 | async-start | bytes 2949120 | tf_op jit(solution)/shard_map/all_gather | solution.py:168
  424.4 31.3 %all-to-all-start.4 = ((bf16[8,12,8]{1,2,0:T(8,128)(2,1)}), bf16[8,12,8]{1,2,0:T(8,128)(2,1)}, u32[]{:S(2)}, u32[]{:S(2)}) async-start(bf16[8,12,8]{1,2,0:T(8,128)(2,1)} %copy.162), calls=%async_computation.8 | async-start | bytes 32768 | tf_op jit(solution)/shard_map/all_to_all | solution.py:20
  455.7 120.5 %all-to-all-start.3 = ((bf16[8,96,768]{2,1,0:T(8,128)(2,1)}), bf16[8,96,768]{2,1,0:T(8,128)(2,1)}, u32[]{:S(2)}, u32[]{:S(2)}) async-start(bf16[8,96,768]{2,1,0:T(8,128)(2,1)} %bitcast.161), calls=%async_computation.7 | async-start | bytes 2359296 | tf_op jit(solution)/shard_map/all_to_all | solution.py:20
  461.7 240.1 %reduce-scatter.11.cloned.1.call-start = ((), (), s32[]{:S(2)}) async-start(), calls=%async_computation.19 | async-start | bytes 2949120 | tf_op jit(solution)/shard_map/reduce_scatter | solution.py:216
  576.1 38.1 %all-to-all-start.5 = ((bf16[8,774,96]{1,2,0:T(8,128)(2,1)}), bf16[8,774,96]{1,2,0:T(8,128)(2,1)S(1)}, u32[]{:S(2)}, u32[]{:S(2)}) async-start(bf16[8,774,96]{1,2,0:T(8,128)(2,1)} %bitcast.149), calls=%async_computation.9 | async-start | bytes 2752512 | tf_op jit(solution)/shard_map/all_to_all | solution.py:20
  582.4 35.5 %copy-start.11 = (bf16[24,8,3,512]{3,1,2,0:T(8,128)(2,1)S(1)}, bf16[24,8,3,512]{3,1,2,0:T(8,128)(2,1)}, u32[]{:S(2)}) copy-start(bf16[24,8,3,512]{3,1,2,0:T(8,128)(2,1)} %copy-done.10) | copy-start | bytes 1769476
  614.3 10.2 %all-to-all-start.1 = ((bf16[8,2,3,8]{3,1,2,0:T(2,128)(2,1)}), bf16[8,2,3,8]{3,1,2,0:T(2,128)(2,1)S(1)}, u32[]{:S(2)}, u32[]{:S(2)}) async-start(bf16[8,2,3,8]{3,1,2,0:T(2,128)(2,1)} %copy.158), calls=%async_computation.5 | async-start | bytes 24576 | tf_op jit(solution)/shard_map/all_to_all | solution.py:20
  624.4 14.4 %all-to-all-start.2 = ((bf16[8,192,96]{2,1,0:T(8,128)(2,1)}), bf16[8,192,96]{2,1,0:T(8,128)(2,1)S(1)}, u32[]{:S(2)}, u32[]{:S(2)}) async-start(bf16[8,192,96]{2,1,0:T(8,128)(2,1)} %bitcast.116), calls=%async_computation.6 | async-start | bytes 786432 | tf_op jit(solution)/shard_map/all_to_all | solution.py:20
  638.8 60.6 %all-to-all-start = ((bf16[8,3,96,192]{2,3,1,0:T(8,128)(2,1)}), bf16[8,3,96,192]{2,3,1,0:T(8,128)(2,1)}, u32[]{:S(2)}, u32[]{:S(2)}) async-start(bf16[8,3,96,192]{2,3,1,0:T(8,128)(2,1)} %bitcast.115), calls=%async_computation.4 | async-start | bytes 2359296 | tf_op jit(solution)/shard_map/all_to_all | solution.py:20
  (57 other events, 217.1 us)
Sparse Core Ops, SparseCore 0:
  10.4 26.7 all-gather.9
  158.3 46.1 reduce-scatter.4
  364.2 47.8 reduce-scatter.8
Sparse Core Ops, SparseCore 1:
  161.0 39.8 all-gather.13
  214.9 21.1 all-gather.11
  238.4 41.3 all-gather.15
  285.2 31.4 reduce-scatter.6
  325.7 23.9 all-gather.17
  419.1 23.9 all-gather.19
  572.6 33.4 reduce-scatter.10
where the time goes:
time: 722 us; the launch traced here: 712 us
  blocking collectives  237 us (33%)
  waiting for transfers between devices  164 us (23%)
  matrix products  135 us (19%)
  other arithmetic  80.1 us (11%)
  local copies, waits for them, and re-layouts  39 us (5%)
  starting transfers between devices  29.6 us (4%)
  between operations  17 us (2%)
  loops' own time  10.2 us (1%)
    reduce_scatter x1, waiting for transfers between devices, shards(): lax.psum_scatter(d_norm_part, 'tensor', scatter_dimension=0, tiled=True)  48 us
    psum x1, blocking collectives, shards(): lax.psum((squares, jnp.sum(local_pad)), ('fsdp', 'tensor'))  45.4 us
    all_gather x1, blocking collectives, shards(): lax.all_gather(attn_weight, 'fsdp', axis=1, tiled=True)  37.9 us
    all_to_all x6, waiting for transfers between devices, summed_on_arrival(): lax.all_to_all(blocks, axis, split_axis=0, concat_axis=0, tiled=True)  36.7 us
    all_gather x1, blocking collectives, shards(): lax.all_gather(query_value_bias, 'fsdp', axis=2, tiled=True)  32.2 us
    all_gather x1, blocking collectives, shards(): lax.all_gather(out_weight, 'fsdp', axis=1, tiled=True)  31.5 us
    reduce_scatter x1, waiting for transfers between devices, shards(): lax.psum_scatter(ff_part.astype(jnp.bfloat16), 'tensor', scatter_dimensio...  30.8 us
    all_to_all x6, starting transfers between devices, summed_on_arrival(): lax.all_to_all(blocks, axis, split_axis=0, concat_axis=0, tiled=True)  28.8 us
  transfers between devices with their start and end apart: 16, of which 7 were waited for; matrix products, arithmetic and copies ran while one was open for 24% of the time, Pallas kernels for 0%

commit v1 on v0

--- a/solution.py
+++ b/solution.py
@@ -1,6 +1,10 @@
+import functools
+
 import jax
 import jax.numpy as jnp
 from jax import lax
+from jax.experimental import pallas as pl
+from jax.experimental.pallas import tpu as pltpu
 from jax.sharding import PartitionSpec as P
 
 D = 768
@@ -8,6 +12,140 @@
 
 
 EPSILON = 1e-12
+F32=jnp.float32; BF=jnp.bfloat16
+BQ=256; BK=256
+
+def dot(a,b,dn=((1,),(0,))):
+    return lax.dot_general(a,b,(dn,((),())),preferred_element_type=F32)
+
+def head_rows(x_t, h):
+    r = lax.broadcasted_iota(jnp.int32, x_t.shape, 0)//DH
+    return jnp.where(r==h, x_t, jnp.zeros_like(x_t))
+def head_cols(x, h):
+    r = lax.broadcasted_iota(jnp.int32, x.shape, 1)//DH
+    return jnp.where(r==h, x, jnp.zeros_like(x))
+
+def fold_max(s): return jnp.max(s.reshape(s.shape[0]//8,8,s.shape[1]),axis=0)
+def fold_sum(s): return jnp.sum(s.reshape(s.shape[0]//8,8,s.shape[1]),axis=0)
+
+def fwd_kernel(heads, bounds, q_ref,k_ref,v_ref,sq_ref,sk_ref,pad_ref, ctx_ref, octx_ref, lse_ref, qt, kh, vt, sc):
+    S=q_ref.shape[0]; W=heads*DH
+    qt[...]=(q_ref[...].astype(F32)*0.125).T.astype(BF)
+    kk=k_ref[...]
+    for h in range(heads): kh[h]=kk[:,h*DH:(h+1)*DH]
+    vt[...]=v_ref[...].astype(F32).T.astype(BF)
+    def qblock(i,_):
+        q0=pl.multiple_of(i*BQ,BQ)
+        lo=bounds[2*i]; hi=bounds[2*i+1]
+        sq=sq_ref[0:1,pl.ds(q0,BQ)]
+        qpos=q0+lax.broadcasted_iota(jnp.int32,(BK,BQ),1)
+        def first(j,c):
+            k0=pl.multiple_of(j*BK,BK)
+            sk=jnp.concatenate([sk_ref[pl.ds(k0,BK),:]]*(BQ//128),axis=1)
+            kpos=k0+lax.broadcasted_iota(jnp.int32,(BK,BQ),0)
+            ok=(sk==sq)|(kpos==qpos)
+            out=[]
+            for h in range(heads):
+                s=jnp.where(ok,dot(kh[h,pl.ds(k0,BK),:],qt[h*DH:(h+1)*DH,pl.ds(q0,BQ)]),-1e30)
+                sc[h,pl.ds(k0,BK),:]=s
+                out.append(jnp.maximum(c[h],fold_max(s)))
+            return tuple(out)
+        m=lax.fori_loop(lo,hi,first,(jnp.full((8,BQ),-3e38,F32),)*heads)
+        m=[jnp.max(x,axis=0,keepdims=True) for x in m]
+        def second(j,c):
+            k0=pl.multiple_of(j*BK,BK)
+            out=[]
+            for h in range(heads):
+                l,acc=c[2*h:2*h+2]
+                p=jnp.exp(sc[h,pl.ds(k0,BK),:]-m[h])
+                out+=[l+fold_sum(p),acc+dot(vt[h*DH:(h+1)*DH,pl.ds(k0,BK)],p.astype(BF))]
+            return tuple(out)
+        c=lax.fori_loop(lo,hi,second,(jnp.zeros((8,BQ),F32),jnp.zeros((DH,BQ),F32))*heads)
+        o=[]
+        for h in range(heads):
+            l,acc=c[2*h:2*h+2]
+            l=jnp.sum(l,axis=0,keepdims=True)
+            lse_ref[h:h+1,pl.ds(q0,BQ)]=m[h]+jnp.log(l)
+            o.append(acc/l)
+        ot=jnp.concatenate(o,axis=0)*pad_ref[0:1,pl.ds(q0,BQ)]
+        octx_ref[:,pl.ds(q0,BQ)]=ot
+        ctx_ref[pl.ds(q0,BQ),:]=ot.T.astype(BF)
+        return 0
+    lax.fori_loop(0,S//BQ,qblock,0)
+
+def attn_fwd(bounds,q,k,v,sq,sk,pad):
+    S,W=q.shape; heads=W//DH
+    vm=pl.BlockSpec(memory_space=pltpu.VMEM)
+    return pl.pallas_call(functools.partial(fwd_kernel,heads),
+        in_specs=[pl.BlockSpec(memory_space=pltpu.SMEM)]+[vm]*6,
+        out_specs=[vm]*3,
+        out_shape=[jax.ShapeDtypeStruct((S,W),BF),jax.ShapeDtypeStruct((W,S),F32),jax.ShapeDtypeStruct((heads,S),F32)],
+        scratch_shapes=[pltpu.VMEM((W,S),BF),pltpu.VMEM((heads,S,DH),BF),pltpu.VMEM((W,S),BF),pltpu.VMEM((heads,S,BQ),F32)],
+        compiler_params=pltpu.CompilerParams(vmem_limit_bytes=56<<20),
+        name="attend_forward")(bounds,q,k,v,sq,sk,pad)
+
+def bwd_kernel(heads, bounds, q_ref,k_ref,v_ref,dc_ref,oct_ref,lse_ref,sq_ref,sk_ref,pad_ref, dqkv_ref, qt, dt, kt, kh, vh, qh, dh, dqt, dsum, dka, dva):
+    S=q_ref.shape[0]; W=heads*DH
+    qs=(q_ref[...].astype(F32)*0.125)
+    qsb=qs.astype(BF); qt[...]=qs.T.astype(BF)
+    kk=k_ref[...]; vv=v_ref[...]
+    kt[...]=kk.astype(F32).T.astype(BF)
+    dct=dc_ref[...].astype(F32).T*pad_ref[0:1,:]
+    dt[...]=dct.astype(BF)
+    dcn=dct.T.astype(BF)
+    prod=dct*oct_ref[...]
+    for h in range(heads):
+        c=slice(h*DH,(h+1)*DH)
+        kh[h]=kk[:,c]; vh[h]=vv[:,c]; qh[h]=qsb[:,c]; dh[h]=dcn[:,c]
+        dsum[h:h+1,:]=jnp.sum(prod[h*DH:(h+1)*DH],axis=0,keepdims=True)
+    dqt[...]=jnp.zeros_like(dqt)
+    def kblock(j,_):
+        k0=pl.multiple_of(j*BK,BK)
+        lo=bounds[2*j]; hi=bounds[2*j+1]
+        sk=jnp.concatenate([sk_ref[pl.ds(k0,BK),:]]*(BQ//128),axis=1)
+        kpos=k0+lax.broadcasted_iota(jnp.int32,(BK,BQ),0)
+        dka[...]=jnp.zeros_like(dka); dva[...]=jnp.zeros_like(dva)
+        def body(i,_):
+            q0=pl.multiple_of(i*BQ,BQ)
+            sq=sq_ref[0:1,pl.ds(q0,BQ)]
+            qpos=q0+lax.broadcasted_iota(jnp.int32,(BK,BQ),1)
+            ok=(sk==sq)|(kpos==qpos)
+            for h in range(heads):
+                r=slice(h*DH,(h+1)*DH)
+                s=jnp.where(ok,dot(kh[h,pl.ds(k0,BK),:],qt[r,pl.ds(q0,BQ)]),-1e30)
+                p=jnp.exp(s-lse_ref[h:h+1,pl.ds(q0,BQ)])
+                dp=dot(vh[h,pl.ds(k0,BK),:],dt[r,pl.ds(q0,BQ)])
+                ds=(p*(dp-dsum[h:h+1,pl.ds(q0,BQ)])).astype(BF)
+                dva[h]+=dot(p.astype(BF),dh[h,pl.ds(q0,BQ),:])
+                dka[h]+=dot(ds,qh[h,pl.ds(q0,BQ),:])
+                dqt[r,pl.ds(q0,BQ)]+=dot(kt[r,pl.ds(k0,BK)],ds)
+            return 0
+        lax.fori_loop(lo,hi,body,0)
+        dqkv_ref[1,pl.ds(k0,BK),:]=jnp.concatenate([dka[h] for h in range(heads)],axis=1).astype(BF)
+        dqkv_ref[2,pl.ds(k0,BK),:]=jnp.concatenate([dva[h] for h in range(heads)],axis=1).astype(BF)
+        return 0
+    lax.fori_loop(0,S//BK,kblock,0)
+    dqkv_ref[0]=(dqt[...]*0.125).T.astype(BF)
+
+def attn_bwd(bounds,q,k,v,dc,oct,lse,sq,sk,pad):
+    S,W=q.shape; heads=W//DH
+    vm=pl.BlockSpec(memory_space=pltpu.VMEM)
+    return pl.pallas_call(functools.partial(bwd_kernel,heads),
+        in_specs=[pl.BlockSpec(memory_space=pltpu.SMEM)]+[vm]*9,
+        out_specs=vm,
+        out_shape=jax.ShapeDtypeStruct((3,S,W),BF),
+        scratch_shapes=[pltpu.VMEM((W,S),BF)]*3+[pltpu.VMEM((heads,S,DH),BF)]*4+[pltpu.VMEM((W,S),F32),pltpu.VMEM((heads,S),F32)]+[pltpu.VMEM((heads,BK,DH),F32)]*2,
+        compiler_params=pltpu.CompilerParams(vmem_limit_bytes=60<<20),
+        name="attend_backward")(bounds,q,k,v,dc,oct,lse,sq,sk,pad)
+
+def side_tables(seg,pad):
+    S=seg.shape[0]; nb=S//BQ
+    skl=jnp.where(pad==1,seg,-1)
+    sk=jnp.broadcast_to(skl[:,None],(S,128))
+    sb=seg.reshape(nb,BQ)
+    lo=jnp.sum((seg[None,:]<sb[:,:1]).astype(jnp.int32),axis=1)//BK
+    hi=(jnp.sum((seg[None,:]<=sb[:,-1:]).astype(jnp.int32),axis=1)+BK-1)//BK
+    return jnp.stack([lo,hi],axis=1).reshape(-1), seg[None,:], sk, pad.astype(F32)[None,:]
 
 
 def split_up(value, dim, devices):
@@ -81,42 +219,13 @@
     heads = width // DH
     projected = jnp.einsum("sd,jde->jse", whole_rows, w_qkv, preferred_element_type=wide)
     qv_flat = qv_full.astype(wide).reshape(2, width)
-    queries = (projected[0] + qv_flat[0]).astype(narrow).reshape(seq_len, heads, DH)
-    all_keys = projected[1].astype(narrow).reshape(seq_len, heads, DH)
-    all_values = (projected[2] + qv_flat[1]).astype(narrow).reshape(seq_len, heads, DH)
-    block_rows = min(512, seq_len)
-    block_count = seq_len // block_rows
-    positions = jnp.arange(seq_len, dtype=jnp.int32)
-    key_live = padding == 1
-
-    def scores_of(row_start):
-        q_rows = lax.dynamic_slice_in_dim(queries, row_start, block_rows, 0)
-        seg_rows = lax.dynamic_slice_in_dim(segment_ids, row_start, block_rows, 0)
-        pos_rows = row_start + jnp.arange(block_rows, dtype=jnp.int32)
-        allowed = (seg_rows[:, None] == segment_ids[None, :]) & key_live[None, :] | (
-            pos_rows[:, None] == positions[None, :]
-        )
-        raw_scores = (
-            jnp.einsum("qhd,khd->hqk", q_rows, all_keys, preferred_element_type=wide) * 0.125
-        )
-        return (q_rows, jnp.where(allowed[None], raw_scores, -1e30))
-
-    def forward_block(block_index):
-        row_start = block_index * block_rows
-        q_rows, masked = scores_of(row_start)
-        row_top = jnp.max(masked, axis=-1, keepdims=True)
-        exp_terms = jnp.exp(masked - row_top)
-        row_total = jnp.sum(exp_terms, axis=-1, keepdims=True)
-        attn_probs = exp_terms / row_total
-        pad_rows = lax.dynamic_slice_in_dim(padding, row_start, block_rows, 0).astype(wide)
-        context = jnp.einsum(
-            "hqk,khd->qhd", attn_probs.astype(narrow), all_values, preferred_element_type=wide
-        )
-        return (context * pad_rows[:, None, None], row_top[..., 0] + jnp.log(row_total[..., 0]))
-
-    block_ids = jnp.arange(block_count, dtype=jnp.int32)
-    contexts, log_totals = lax.map(forward_block, block_ids)
-    context_low = contexts.reshape(seq_len, width).astype(narrow)
+    queries = (projected[0] + qv_flat[0]).astype(narrow)
+    all_keys = projected[1].astype(narrow)
+    all_values = (projected[2] + qv_flat[1]).astype(narrow)
+    bounds, seg_row, seg_keys, pad_row = side_tables(segment_ids, padding)
+    context_low, context_t, log_totals = attn_fwd(
+        bounds, queries, all_keys, all_values, seg_row, seg_keys, pad_row
+    )
     attn_part = jnp.dot(context_low, w_proj, preferred_element_type=wide)
     attn_branch = lax.psum_scatter(
         attn_part, "tensor", scatter_dimension=0, tiled=True
@@ -170,43 +279,10 @@
     d_context = jnp.einsum("sd,ed->se", d_attn_all, w_proj, preferred_element_type=wide).astype(
         narrow
     )
-    d_context = d_context.reshape(seq_len, heads, DH)
-
-    def backward_block(carried, block_index):
-        d_keys_sum, d_values_sum = carried
-        row_start = block_index * block_rows
-        q_rows, masked = scores_of(row_start)
-        attn_probs = jnp.exp(masked - log_totals[block_index][..., None])
-        pad_rows = lax.dynamic_slice_in_dim(padding, row_start, block_rows, 0).astype(narrow)
-        d_ctx_rows = (
-            lax.dynamic_slice_in_dim(d_context, row_start, block_rows, 0) * pad_rows[:, None, None]
-        )
-        d_probs = jnp.einsum("qhd,khd->hqk", d_ctx_rows, all_values, preferred_element_type=wide)
-        d_values_sum = d_values_sum + jnp.einsum(
-            "hqk,qhd->khd", attn_probs.astype(narrow), d_ctx_rows, preferred_element_type=wide
-        )
-        inner_sum = jnp.sum(attn_probs * d_probs, axis=-1, keepdims=True)
-        d_scores = (attn_probs * (d_probs - inner_sum)).astype(narrow)
-        d_query_rows = (
-            jnp.einsum("hqk,khd->qhd", d_scores, all_keys, preferred_element_type=wide) * 0.125
-        )
-        d_keys_sum = (
-            d_keys_sum
-            + jnp.einsum("hqk,qhd->khd", d_scores, q_rows, preferred_element_type=wide) * 0.125
-        )
-        return ((d_keys_sum, d_values_sum), d_query_rows)
-
-    zero_heads = jnp.zeros((seq_len, heads, DH), wide)
-    (d_keys_all, d_values_all), d_query_blocks = lax.scan(
-        backward_block, (zero_heads, zero_heads), block_ids
-    )
-    d_qkv = jnp.stack(
-        [
-            d_query_blocks.reshape(seq_len, width),
-            d_keys_all.reshape(seq_len, width),
-            d_values_all.reshape(seq_len, width),
-        ]
-    ).astype(narrow)
+    d_qkv = attn_bwd(
+        bounds, queries, all_keys, all_values, d_context, context_t, log_totals,
+        seg_row, seg_keys, pad_row,
+    )
     d_qkv_wide = d_qkv.astype(wide)
     d_qv_bias = jnp.stack([jnp.sum(d_qkv_wide[0], axis=0), jnp.sum(d_qkv_wide[2], axis=0)]).reshape(
         2, heads, DH

time: 722 us -> 623 us (0.86)
  matrix products: 135 us -> 68.3 us
  other arithmetic: 80.1 us -> 32.6 us
  Pallas kernels: 0 us -> 38.7 us
  loops' own time: 10.2 us -> 0 us
    dot_general x21 -> x0, matrix products: 71.7 us -> none  [the longest x6 27.7 us: scores_of(): jnp.einsum('qhd,khd->hqk', q_rows, all_keys, preferred_element_type=wide)]
    pallas_call x0 -> x2, Pallas kernels: none -> 38.7 us  [the longest x1 23.9 us: attn_bwd(): pl.pallas_call(functools.partial(bwd_kernel, heads), in_specs=[pl.BlockSp...]
    convert_element_type x10 -> x2, other arithmetic: 31 us -> 2.33 us  [the longest x1 1.53 us: shards(): all_values = (projected[2] + qv_flat[1]).astype(narrow)]
    another operation x2 -> x0, loops' own time: 10.2 us -> none  [the longest x1 8.2 us: shards(): lax.scan(backward_block, (zero_heads, zero_heads), block_ids)]
    reduce_sum x3 -> x1, other arithmetic: 8.39 us -> 0.93 us  [side_tables(): lo = jnp.sum((seg[None, :] < sb[:, :1]).astype(jnp.int32), axis=1) // BK]
  transfers between devices with their start and end apart: 16 -> 16, of which waited for: 7 -> 7; matrix products, arithmetic and copies ran while one was open for 24% -> 14% of each run, Pallas kernels for 0% -> 4%
where the time goes in v1:
time: 623 us; the launch traced here: 614 us
  blocking collectives  238 us (38%)
  waiting for transfers between devices  158 us (25%)
  matrix products  68.3 us (11%)
  Pallas kernels  38.7 us (6%)
  other arithmetic  32.6 us (5%)
  local copies, waits for them, and re-layouts  32.2 us (5%)
  starting transfers between devices  30.2 us (5%)
  between operations  16.8 us (3%)
    reduce_scatter x1, waiting for transfers between devices, shards(): lax.psum_scatter(d_norm_part, 'tensor', scatter_dimension=0, tiled=True)  47.9 us
    psum x1, blocking collectives, shards(): lax.psum((squares, jnp.sum(local_pad)), ('fsdp', 'tensor'))  45.7 us
    all_gather x1, blocking collectives, shards(): lax.all_gather(attn_weight, 'fsdp', axis=1, tiled=True)  38.4 us
    all_gather x1, blocking collectives, shards(): lax.all_gather(query_value_bias, 'fsdp', axis=2, tiled=True)  32.2 us
    all_gather x1, blocking collectives, shards(): lax.all_gather(out_weight, 'fsdp', axis=1, tiled=True)  31.5 us
    all_to_all x6, waiting for transfers between devices, summed_on_arrival(): lax.all_to_all(blocks, axis, split_axis=0, concat_axis=0, tiled=True)  31 us
    reduce_scatter x1, waiting for transfers between devices, shards(): lax.psum_scatter(ff_part.astype(jnp.bfloat16), 'tensor', scatter_dimensio...  30.1 us
    all_to_all x6, starting transfers between devices, summed_on_arrival(): lax.all_to_all(blocks, axis, split_axis=0, concat_axis=0, tiled=True)  29.6 us
  transfers between devices with their start and end apart: 16, of which 7 were waited for; matrix products, arithmetic and copies ran while one was open for 14% of the time, Pallas kernels for 4%

profile of v1, /device:TPU:0, one launch (start us, length us, event | category | flops | bytes accessed | tf_op | source)
XLA Modules:
  0.0 613.9 jit_solution(11681134377471513369)
XLA Ops:
  14.4 32.2 %all_gather.41 = bf16[2,3,64]{1,0,2:T(2,128)(2,1)S(1)} all-gather(bf16[2,3,8]{1,0,2:T(2,128)(2,1)S(1)} %copy.209), channel_id=1, replica_groups=mesh['fsdp'=8,'tensor'=4] {'fsdp'}, dimensions={2}, use_global_device_ids=true | all-gather | bytes 864 | tf_op jit(solution)/shard_map/all_gather | solution.py:201
  49.3 31.5 %all_gather.42 = bf16[192,768]{0,1:T(8,128)(2,1)S(1)} all-gather(bf16[192,96]{0,1:T(8,128)(2,1)S(1)} %copy.212), channel_id=1, replica_groups=mesh['fsdp'=8,'tensor'=4] {'fsdp'}, dimensions={1}, use_global_device_ids=true | all-gather | bytes 331776 | tf_op jit(solution)/shard_map/all_gather | solution.py:202
  80.8 38.4 %all_gather.39 = bf16[3,768,192]{2,0,1:T(4,128)(2,1)S(1)} all-gather(bf16[3,96,192]{2,0,1:T(4,128)(2,1)S(1)} %copy.206), channel_id=1, replica_groups=mesh['fsdp'=8,'tensor'=4] {'fsdp'}, dimensions={1}, use_global_device_ids=true | all-gather | bytes 995328 | tf_op jit(solution)/shard_map/all_gather | solution.py:200
  127.2 14.8 %attend_forward.1 = (bf16[1536,192]{1,0:T(8,128)(2,1)}, f32[192,1536]{1,0:T(8,128)}, f32[3,1536]{1,0:T(4,128)}) custom-call(s32[12]{0:T(128)} %reshape.240.bounds, bf16[1536,192]{1,0:T(8,128)(2,1)} %get-tuple-element.172.q_ref, bf16[1536,192]{1,0:T(8,128)(2,1)} %fusion.30.k_ref, bf16[1536,192]{1,0:T(8,128)(2,1)} %get-tuple-element.171.v_ref, ...), custom_call_target="tpu_custom_call" | custom-call | tf_op jit(solution)/shard_map/attend_forward/pallas_call | solution.py:79
  146.8 18.0 %all-gather = bf16[8,96,2]{1,2,0:T(2,128)(2,1)S(1)} all-gather(bf16[1,96,2]{1,2,0:T(2,128)(2,1)S(1)} %bitcast.107), channel_id=1, replica_groups=mesh['fsdp'=8,'tensor'=4] {'fsdp'}, dimensions={0}, use_global_device_ids=true | all-gather | bytes 3456 | tf_op jit(solution)/shard_map/all_gather | solution.py:208
  164.8 16.5 %all-gather.1 = bf16[8,96,2]{1,2,0:T(2,128)(2,1)S(1)} all-gather(bf16[1,96,2]{1,2,0:T(2,128)(2,1)S(1)} %bitcast.108), channel_id=1, replica_groups=mesh['fsdp'=8,'tensor'=4] {'fsdp'}, dimensions={0}, use_global_device_ids=true | all-gather | bytes 3456 | tf_op jit(solution)/shard_map/all_gather | solution.py:206
  181.4 17.8 %all-gather.2 = bf16[8,96,2]{1,2,0:T(2,128)(2,1)S(1)} all-gather(bf16[1,96,2]{1,2,0:T(2,128)(2,1)S(1)} %bitcast.109), channel_id=1, replica_groups=mesh['fsdp'=8,'tensor'=4] {'fsdp'}, dimensions={0}, use_global_device_ids=true | all-gather | bytes 3456 | tf_op jit(solution)/shard_map/all_gather | solution.py:207
  203.6 26.2 %all_gather.48 = bf16[12,64]{0,1:T(8,128)(2,1)S(1)} all-gather(bf16[12,8]{0,1:T(8,128)(2,1)S(1)} %copy-done.16), channel_id=1, replica_groups=mesh['fsdp'=8,'tensor'=4] {'fsdp'}, dimensions={1}, use_global_device_ids=true | all-gather | bytes 1728 | tf_op jit(solution)/shard_map/all_gather | solution.py:204
  229.9 15.2 %multiply_convert_fusion = (bf16[1536,768]{1,0:T(8,128)(2,1)}, f32[1536,768]{1,0:T(8,128)}, f32[1536,768]{1,0:T(8,128)}) fusion(f32[768]{0:T(1024)S(1)} %reshape.252, bf16[1536,768]{1,0:T(8,128)(2,1)} %all-gather.12.cloned.1.call-done, bf16[768,768]{1,0:T(8,128)(2,1)} %all-gather.14.cloned.1.call-done), kind=kOutput, calls=%fused_computation.4 | convolution fusion | flops 1889796096 | bytes 15338496 | tf_op jit(solution)/shard_map/dot_general | solution.py:239
  245.1 22.9 %all-gather.16.cloned.1.call-done = bf16[768,768]{0,1:T(8,128)(2,1)} async-done(((bf16[768,96]{0,1:T(8,128)(2,1)}), bf16[768,768]{0,1:T(8,128)(2,1)}) %all-gather.16.cloned.1.call-update) | async-done | bytes 1179664 | tf_op jit(solution)/shard_map/all_gather | solution.py:205
  268.0 5.4 convolution_convert_fusion
  275.0 30.1 %reduce-scatter.7.cloned.1.call-done = bf16[384,768]{1,0:T(8,128)(2,1)} async-done(((bf16[1536,768]{1,0:T(8,128)(2,1)}), bf16[384,768]{1,0:T(8,128)(2,1)}) %reduce-scatter.7.cloned.1.call-update) | async-done | bytes 589840 | tf_op jit(solution)/shard_map/reduce_scatter | solution.py:245
  311.5 23.8 %all-gather.18.cloned.1.call-done = bf16[1536,768]{1,0:T(8,128)(2,1)} async-done(((bf16[384,768]{1,0:T(8,128)(2,1)}), bf16[1536,768]{1,0:T(8,128)(2,1)}) %all-gather.18.cloned.1.call-update) | async-done | bytes 2359312 | tf_op jit(solution)/shard_map/all_gather | solution.py:266
  335.2 8.2 %fusion.40 = (bf16[768]{0:T(1024)(128)(2,1)S(1)}, bf16[1536,768]{1,0:T(8,128)(2,1)S(1)}) fusion(f32[1536,768]{1,0:T(8,128)} %get-tuple-element.168, f32[1536,768]{1,0:T(8,128)} %get-tuple-element.183, f32[768]{0:T(1024)S(1)} %copy-done.15, bf16[1536,768]{1,0:T(8,128)(2,1)} %all-gather.18.cloned.1.call-done, bf16[768,768]{0,1:T(8,128)(2,1)} %all-gather.16.cloned.1.call-done), kind=kOutput, calls=%fused_computation.127 | convolution fusion | flops 1830812928 | bytes 15340032 | tf_op jit(solution)/shard_map/sd,fd->sf/dot_general | solution.py:268
  349.2 47.9 %reduce-scatter.9.cloned.1.call-done = f32[384,768]{1,0:T(8,128)} async-done(((f32[1536,768]{1,0:T(8,128)}), f32[384,768]{1,0:T(8,128)}) %reduce-scatter.9.cloned.1.call-update) | async-done | bytes 1179664 | tf_op jit(solution)/shard_map/reduce_scatter | solution.py:273
  402.1 5.5 all-to-all-start.4
  407.6 6.0 convolution_convert_fusion.3
  414.2 5.4 all-to-all-start.3
  419.7 5.5 convolution_convert_fusion.2
  425.3 11.3 %all-reduce.1 = (bf16[2,768]{1,0:T(2,128)(2,1)S(1)}, bf16[2,768]{1,0:T(2,128)(2,1)S(1)}, bf16[2,768]{1,0:T(2,128)(2,1)S(1)}) all-reduce(f32[2,768]{1,0:T(2,128)S(1)} %pad_maximum_fusion.3, f32[2,768]{1,0:T(2,128)S(1)} %pad_maximum_fusion.2, f32[2,768]{1,0:T(2,128)S(1)} %pad_maximum_fusion.1), channel_id=1, replica_groups=mesh['fsdp'=8,'tensor'=4] {'tensor'}, use_global_device_ids=true, to_apply=%region_30.31 | all-reduce | flops 4608 | bytes 27648 | tf_op jit(solution)/shard_map/psum | solution.py:295
  440.5 23.9 %attend_backward.1 = bf16[3,1536,192]{2,1,0:T(8,128)(2,1)} custom-call(s32[12]{0:T(128)} %reshape.240.bounds, bf16[1536,192]{1,0:T(8,128)(2,1)} %get-tuple-element.172.q_ref, bf16[1536,192]{1,0:T(8,128)(2,1)} %fusion.30.k_ref, bf16[1536,192]{1,0:T(8,128)(2,1)} %get-tuple-element.171.v_ref, bf16[1536,192]{1,0:T(8,128)(2,1)} %copy.217.dc_ref, ...), custom_call_target="tpu_custom_call" | custom-call | tf_op jit(solution)/shard_map/attend_backward/pallas_call | solution.py:133
  484.8 27.2 %all-to-all-done.5 = bf16[8,774,96]{1,2,0:T(8,128)(2,1)} async-done(((bf16[8,774,96]{1,2,0:T(8,128)(2,1)}), bf16[8,774,96]{1,2,0:T(8,128)(2,1)}, u32[]{:S(2)}, u32[]{:S(2)}) %all-to-all-start.5) | async-done | bytes 1188896 | tf_op jit(solution)/shard_map/all_to_all | solution.py:158
  523.2 5.9 all-to-all-start.2
  545.9 45.7 %all-reduce = (f32[3]{0:T(128)S(1)}, f32[]{:T(128)}) all-reduce(f32[3]{0:T(128)S(1)} %pad_maximum_fusion.4, f32[]{:T(128)} %get-tuple-element.152), channel_id=1, replica_groups=mesh['fsdp'=8,'tensor'=4] {'fsdp','tensor'}, use_global_device_ids=true, to_apply=%region_35.36 | all-reduce | flops 4 | bytes 32 | tf_op jit(solution)/shard_map/psum | solution.py:261
  (177 shorter events, 111.6 us)
Async XLA Ops:
  8.0 111.2 %all-gather.10.cloned.1.call-start = ((), (), s32[]{:S(2)}) async-start(), calls=%async_computation.10 | async-start | bytes 2949120 | tf_op jit(solution)/shard_map/all_gather | solution.py:217
  8.7 191.3 %reduce-scatter.5.cloned.1.call-start = ((), (), s32[]{:S(2)}) async-start(), calls=%async_computation.11 | async-start | bytes 5898240 | tf_op jit(solution)/shard_map/reduce_scatter | solution.py:230
  80.8 61.3 %copy-start.3 = (bf16[192,768]{0,1:T(8,128)(2,1)}, bf16[192,768]{0,1:T(8,128)(2,1)S(1)}, u32[]{:S(2)}) copy-start(bf16[192,768]{0,1:T(8,128)(2,1)S(1)} %all_gather.42) | copy-start | bytes 884740
  146.1 18.7 %copy-start.18 = (bf16[2,96]{1,0:T(2,128)(2,1)S(1)}, bf16[2,96]{1,0:T(2,128)(2,1)}, u32[]{:S(2)}) copy-start(bf16[2,96]{1,0:T(2,128)(2,1)} %param.20) | copy-start | bytes 1156
  146.1 35.3 %copy-start.19 = (bf16[2,96]{1,0:T(2,128)(2,1)S(1)}, bf16[2,96]{1,0:T(2,128)(2,1)}, u32[]{:S(2)}) copy-start(bf16[2,96]{1,0:T(2,128)(2,1)} %param.21) | copy-start | bytes 1156
  146.1 53.9 %copy-start.1 = (bf16[384,768]{1,0:T(8,128)(2,1)S(1)}, bf16[384,768]{1,0:T(8,128)(2,1)}, u32[]{:S(2)}) copy-start(bf16[384,768]{1,0:T(8,128)(2,1)} %param.13) | copy-start | bytes 1769476
  146.1 83.8 %all-gather.14.cloned.1.call-start = ((), (), s32[]{:S(2)}) async-start(), calls=%async_computation.13 | async-start | bytes 1327104 | tf_op jit(solution)/shard_map/all_gather | solution.py:203
  146.7 83.2 %all-gather.12.cloned.1.call-start = ((), (), s32[]{:S(2)}) async-start(), calls=%async_computation.12 | async-start | bytes 2949120 | tf_op jit(solution)/shard_map/all_gather | solution.py:238
  202.9 65.1 %all-gather.16.cloned.1.call-start = ((), (), s32[]{:S(2)}) async-start(), calls=%async_computation.14 | async-start | bytes 1327104 | tf_op jit(solution)/shard_map/all_gather | solution.py:205
  203.5 101.6 %reduce-scatter.7.cloned.1.call-start = ((), (), s32[]{:S(2)}) async-start(), calls=%async_computation.15 | async-start | bytes 2949120 | tf_op jit(solution)/shard_map/reduce_scatter | solution.py:245
  273.5 31.6 %copy-start.2 = (f32[384,768]{1,0:T(8,128)S(1)}, f32[384,768]{1,0:T(8,128)}, u32[]{:S(2)}) copy-start(f32[384,768]{1,0:T(8,128)} %reduce-scatter.5.cloned.1.call-done) | copy-start | bytes 3538948
  273.5 61.7 %all-gather.18.cloned.1.call-start = ((), (), s32[]{:S(2)}) async-start(), calls=%async_computation.16 | async-start | bytes 2949120 | tf_op jit(solution)/shard_map/all_gather | solution.py:266
  308.8 26.4 %copy-start.15 = (f32[768]{0:T(1024)S(1)}, f32[768]{0:T(1024)}, u32[]{:S(2)}) copy-start(f32[768]{0:T(1024)} %copy-done.14) | copy-start | bytes 9220
  311.2 86.0 %reduce-scatter.9.cloned.1.call-start = ((), (), s32[]{:S(2)}) async-start(), calls=%async_computation.17 | async-start | bytes 5898240 | tf_op jit(solution)/shard_map/reduce_scatter | solution.py:273
  349.1 49.9 %copy-start.10 = (f32[384]{0:T(512)S(1)}, f32[384]{0:T(512)}, u32[]{:S(2)}) copy-start(f32[384]{0:T(512)} %copy-done.9) | copy-start | bytes 4612
  349.2 87.5 %all-gather.20.cloned.1.call-start = ((), (), s32[]{:S(2)}) async-start(), calls=%async_computation.18 | async-start | bytes 2949120 | tf_op jit(solution)/shard_map/all_gather | solution.py:277
  402.1 12.1 %all-to-all-start.4 = ((bf16[8,12,8]{1,2,0:T(8,128)(2,1)}), bf16[8,12,8]{1,2,0:T(8,128)(2,1)S(1)}, u32[]{:S(2)}, u32[]{:S(2)}) async-start(bf16[8,12,8]{1,2,0:T(8,128)(2,1)} %copy.227), calls=%async_computation.8 | async-start | bytes 32768 | tf_op jit(solution)/shard_map/all_to_all | solution.py:158
  414.2 60.3 %all-to-all-start.3 = ((bf16[8,96,768]{2,1,0:T(8,128)(2,1)}), bf16[8,96,768]{2,1,0:T(8,128)(2,1)}, u32[]{:S(2)}, u32[]{:S(2)}) async-start(bf16[8,96,768]{2,1,0:T(8,128)(2,1)} %bitcast.21), calls=%async_computation.7 | async-start | bytes 2359296 | tf_op jit(solution)/shard_map/all_to_all | solution.py:158
  419.6 184.5 %reduce-scatter.11.cloned.1.call-start = ((), (), s32[]{:S(2)}) async-start(), calls=%async_computation.19 | async-start | bytes 2949120 | tf_op jit(solution)/shard_map/reduce_scatter | solution.py:292
  440.5 23.9 %copy-start.7 = (bf16[3,768,192]{2,0,1:T(4,128)(2,1)S(1)}, bf16[3,768,192]{2,0,1:T(4,128)(2,1)}, u32[]{:S(2)}) copy-start(bf16[3,768,192]{2,0,1:T(4,128)(2,1)} %copy-done.6) | copy-start | bytes 2654212
  474.5 37.5 %all-to-all-start.5 = ((bf16[8,774,96]{1,2,0:T(8,128)(2,1)}), bf16[8,774,96]{1,2,0:T(8,128)(2,1)}, u32[]{:S(2)}, u32[]{:S(2)}) async-start(bf16[8,774,96]{1,2,0:T(8,128)(2,1)} %bitcast.101), calls=%async_computation.9 | async-start | bytes 2752512 | tf_op jit(solution)/shard_map/all_to_all | solution.py:158
  512.0 11.2 %all-to-all-start.1 = ((bf16[8,2,3,8]{3,1,2,0:T(2,128)(2,1)}), bf16[8,2,3,8]{3,1,2,0:T(2,128)(2,1)}, u32[]{:S(2)}, u32[]{:S(2)}) async-start(bf16[8,2,3,8]{3,1,2,0:T(2,128)(2,1)} %copy.223), calls=%async_computation.5 | async-start | bytes 24576 | tf_op jit(solution)/shard_map/all_to_all | solution.py:158
  523.2 17.1 %all-to-all-start.2 = ((bf16[8,192,96]{2,1,0:T(8,128)(2,1)}), bf16[8,192,96]{2,1,0:T(8,128)(2,1)}, u32[]{:S(2)}, u32[]{:S(2)}) async-start(bf16[8,192,96]{2,1,0:T(8,128)(2,1)} %bitcast.102), calls=%async_computation.6 | async-start | bytes 786432 | tf_op jit(solution)/shard_map/all_to_all | solution.py:158
  540.3 62.7 %all-to-all-start = ((bf16[8,3,96,192]{2,3,1,0:T(8,128)(2,1)}), bf16[8,3,96,192]{2,3,1,0:T(8,128)(2,1)S(1)}, u32[]{:S(2)}, u32[]{:S(2)}) async-start(bf16[8,3,96,192]{2,3,1,0:T(8,128)(2,1)} %bitcast.99), calls=%async_computation.4 | async-start | bytes 2359296 | tf_op jit(solution)/shard_map/all_to_all | solution.py:158
  (14 other events, 74.1 us)
Sparse Core Ops, SparseCore 0:
  10.4 26.7 all-gather.9
  146.3 46.8 reduce-scatter.4
  349.3 47.8 reduce-scatter.8
Sparse Core Ops, SparseCore 1:
  149.0 40.3 all-gather.13
  203.0 21.1 all-gather.11
  226.5 41.5 all-gather.15
  273.6 31.4 reduce-scatter.6
  311.3 23.9 all-gather.17
  401.3 23.9 all-gather.19
  469.6 32.4 reduce-scatter.10
